TPU v7x, 32 devices: a whole 2x2x4 slice. The times are simulated.
32 devices in a mesh: pb: 4 (over z), freq: 4 (over y, core), ga: 2 (over x).
Axes of the slice: x: 2, y: 2, z: 4, core: 2. Of those that a mesh axis runs over, the one named last changes fastest.
Arguments:
- densities: bfloat16 [4, 2, 256, 4096], P('pb', None, ('freq', 'ga')), may hold values from -0.5 to 0.5
- screened: bfloat16 [4, 4, 2, 4096, 4096], P('pb', 'freq', None, 'ga'), may hold values from -0.09375 to 0.09375
- energies: float32 [16, 256], replicated, may hold values from -2.5 to 2.5
- occupied: int32 [16], replicated, may hold values from 64 to 192
- kmq: int32 [4], replicated, may hold values from 0 to 15
- offsets: int32 [4], replicated, may hold values from -16 to 15
- weights: float32 [4], replicated, may hold values from 0.5 to 2
Outputs:
- sigma: float32 [2, 1, 64], P(None, None, ('pb', 'freq'))
All inputs are finite; a program needn't handle non-finite values.
Results may differ from a plain program's by a relative error of at most 0.0003.
Values may be sent and summed in bfloat16 or wider, within the bound.
A program may use at most 64 MiB of HBM per device.

v0:
```python
import math

import jax
import jax.numpy as jnp
from jax import lax
from jax.sharding import PartitionSpec as P

NB = 256
NS = 1
OUT_DEV = 4


broadening = 0.15


def from_behind(block, axis, distance):
    devices = range(lax.axis_size(axis))
    route = [((i - distance) % len(devices), i) for i in devices]
    return lax.ppermute(block, axis, route)


def green_parts(level_row, filled, freq_shift, omegas):
    bands = jnp.arange(level_row.shape[0], dtype=jnp.int32)
    pole_sign = jnp.where(bands < filled, -1.0, 1.0).astype(jnp.float32)
    real_part = omegas[None, :] - freq_shift - level_row[:, None]
    imag_part = broadening * pole_sign[:, None]
    denominator = real_part * real_part + imag_part * imag_part
    return (real_part / denominator, -imag_part / denominator)


def spectrum(pair_real, pair_imag, green_real, green_imag):
    exact = lax.Precision.HIGHEST
    real_out = jnp.dot(pair_real, green_real, precision=exact) - jnp.dot(
        pair_imag, green_imag, precision=exact
    )
    imag_out = jnp.dot(pair_real, green_imag, precision=exact) + jnp.dot(
        pair_imag, green_real, precision=exact
    )
    return jnp.stack([real_out, imag_out])


def panel_product(density_all, screen):
    pair_rows = density_all.shape[1]
    panel_rows = screen.shape[1]
    product = lax.dot_general(
        density_all.reshape(2 * pair_rows, -1),
        screen.reshape(2 * panel_rows, -1),
        (((1,), (1,)), ((), ())),
        preferred_element_type=jnp.float32,
    )
    product = product.reshape(2, pair_rows, 2, panel_rows)
    return (product[0, :, 0] - product[1, :, 1], product[0, :, 1] + product[1, :, 0])


def body(densities, screened, energies, occupied, kmq, offsets, weights):
    qpoint = lax.axis_index("pb")
    my_freq = lax.axis_index("freq")
    my_panel = lax.axis_index("ga")
    count_pb = lax.axis_size("pb")
    count_freq = lax.axis_size("freq")
    screen = screened[0, 0]
    panel_width = screen.shape[1]
    local_block = densities[0]
    whole = lax.all_gather(local_block, ("freq", "ga"), axis=1, tiled=True)
    real_x, imag_x = panel_product(whole, screen)
    own_rows = lax.dynamic_slice_in_dim(whole, my_panel * panel_width, panel_width, 2)
    dense = own_rows.astype(jnp.float32)
    real_sum = jnp.sum(dense[0] * real_x + dense[1] * imag_x, axis=1)
    imag_sum = jnp.sum(dense[0] * imag_x - dense[1] * real_x, axis=1)
    pair_total = lax.psum(jnp.stack([real_sum, imag_sum]), "ga")
    weighted = (pair_total * weights[my_freq]).reshape(2, NS, NB)
    kpoint = kmq[qpoint]
    level_row = energies[kpoint]
    filled = occupied[kpoint]
    total_out = OUT_DEV * count_pb * count_freq
    index_grid = (jnp.arange(count_pb, dtype=jnp.int32)[:, None] * count_freq + my_freq) * OUT_DEV
    index_grid = (index_grid + jnp.arange(OUT_DEV, dtype=jnp.int32)[None, :]).reshape(-1)
    omegas = -2.0 + 4.0 * index_grid.astype(jnp.float32) / total_out
    summed = jnp.zeros((2, NS, count_pb * OUT_DEV), jnp.float32)
    passed = weighted
    for rotation in range(count_freq):
        anchor = (my_freq - rotation) % count_freq
        freq_shift = 4.0 * offsets[anchor].astype(jnp.float32) / total_out
        green_real, green_imag = green_parts(level_row, filled, freq_shift, omegas)
        summed = summed + spectrum(passed[0], passed[1], green_real, green_imag)
        if rotation + 1 < count_freq:
            passed = from_behind(passed, "freq", 1)
    local_part = lax.psum_scatter(summed, "pb", scatter_dimension=2, tiled=True)
    prefactor = 1.0 / (2.0 * math.pi * count_pb)
    return jnp.stack([-prefactor * local_part[1], prefactor * local_part[0]])


def solution(mesh):
    placed = (
        P("pb", None, ("freq", "ga"), None),
        P("pb", "freq", None, "ga", None),
        P(),
        P(),
        P(),
        P(),
        P(),
    )
    return jax.shard_map(
        body, mesh=mesh, in_specs=placed, out_specs=P(None, None, ("pb", "freq")), check_vma=False
    )
```

profile of v0, /device:TPU:0, one launch (start us, length us, event | category | flops | bytes accessed | tf_op | source)
XLA Modules:
  0.0 112.7 jit_solution(8596917107336101058)
XLA Ops:
  6.5 0.7 all-gather.3.cloned.1.call-update
  7.3 1.2 %dynamic_slice.30 = s32[1]{0:T(128)} dynamic-slice(s32[4]{0:T(128)} %param.11, s32[]{:T(128)S(6)} %select_n.62), dynamic_slice_sizes={1} | dynamic-slice | bytes 12 | tf_op jit(solution)/shard_map/dynamic_slice | solution.py:72
  9.9 1.5 %fusion.102 = (s32[1]{0:T(128)}, s32[1]{0:T(128)}, s32[1]{0:T(128)}, s32[1]{0:T(128)}) fusion(s32[4]{0:T(128)} %param.12, s32[]{:T(128)S(6)} %select_n.70, s32[]{:T(128)S(6)} %select_n.66, s32[]{:T(128)S(6)} %select_n.61, s32[]{:T(128)S(6)} %select_n.68), kind=kLoop, calls=%fused_computation.143 | loop fusion | bytes 48 | tf_op jit(solution)/shard_map/dynamic_slice | solution.py:83
  14.2 1.3 %dynamic-slice.1 = u32[1]{0:T(128)} dynamic-slice(u32[32]{0:T(128)} %constant.95, u32[]{:T(128)S(6)} %add.222), dynamic_slice_sizes={1} | dynamic-slice | bytes 12
  16.1 1.3 %dynamic_slice.28 = f32[1]{0:T(128)} dynamic-slice(f32[4]{0:T(128)} %param.13, s32[]{:T(128)S(6)} %select_n.59), dynamic_slice_sizes={1} | dynamic-slice | bytes 12 | tf_op jit(solution)/shard_map/dynamic_slice | solution.py:71
  18.1 1.2 %dynamic_slice.32 = s32[1]{0:T(128)} dynamic-slice(s32[16]{0:T(128)} %param.10, s32[]{:T(128)S(6)} %select_n.63), dynamic_slice_sizes={1} | dynamic-slice | bytes 12 | tf_op jit(solution)/shard_map/dynamic_slice | solution.py:74
  19.3 0.7 fusion.100
  20.0 28.6 %all-gather.3.cloned.1.call-done = bf16[1,2,256,4096]{3,2,1,0:T(8,128)(2,1)} async-done(((bf16[1,2,32,4096]{3,2,1,0:T(8,128)(2,1)}), bf16[1,2,256,4096]{3,2,1,0:T(8,128)(2,1)}) %all-gather.3.cloned.1.call-update) | async-done | bytes 4194320 | tf_op jit(solution)/shard_map/all_gather | solution.py:64
  48.6 2.1 %dynamic-slice_convert_fusion = f32[1,2,256,2048]{3,2,1,0:T(8,128)S(1)} fusion(bf16[1,2,256,4096]{3,2,1,0:T(8,128)(2,1)} %all-gather.3.cloned.1.call-done, s32[]{:T(128)S(6)} %select_n.58), kind=kLoop, calls=%fused_computation.9 | loop fusion | flops 1048576 | bytes 6291460 | tf_op jit(solution)/shard_map/convert_element_type | solution.py:67
  50.7 22.8 %fusion = f32[2,256,2,2048]{3,1,2,0:T(8,128)S(1)} fusion(bf16[1,1,2,2048,4096]{4,3,2,1,0:T(8,128)(2,1)} %param.8, bf16[1,2,256,4096]{3,2,1,0:T(8,128)(2,1)} %all-gather.3.cloned.1.call-done), kind=kOutput, calls=%fused_computation | convolution fusion | flops 17179869184 | bytes 46137344 | tf_op jit(solution)/shard_map/dot_general | solution.py:45
  73.5 1.2 %add_reduce_fusion = (f32[256]{0:T(256)S(1)}, f32[256]{0:T(256)S(1)}) fusion(f32[1,2,256,2048]{3,2,1,0:T(8,128)S(1)} %dynamic-slice_convert_fusion, f32[2,256,2,2048]{3,1,2,0:T(8,128)S(1)} %fusion), kind=kLoop, calls=%fused_computation.11 | loop fusion | flops 5242368 | bytes 12584960 | tf_op jit(solution)/shard_map/reduce_sum | solution.py:68
  74.7 4.9 %psum.7 = f32[2,256]{1,0:T(2,128)S(1)} all-reduce(f32[2,256]{1,0:T(2,128)S(1)} %pad_maximum_fusion), channel_id=1, replica_groups=mesh['pb'=4,'freq'=4,'ga'=2] {'ga'}, use_global_device_ids=true, to_apply=%region_2.0 | all-reduce | flops 512 | bytes 4096 | tf_op jit(solution)/shard_map/psum | solution.py:70
  79.7 0.6 broadcast_multiply_fusion
  80.3 0.6 fusion.103
  81.5 0.3 fusion.13
  82.2 2.7 %collective-permute-done = f32[2,1,256]{2,0,1:T(2,128)S(1)} collective-permute-done((f32[2,1,256]{2,0,1:T(2,128)S(1)}, f32[2,1,256]{2,0,1:T(2,128)S(1)}, u32[]{:S(2)}, u32[]{:S(2)}) %collective-permute-start) | collective-permute-done | bytes 2080 | tf_op jit(solution)/shard_map/ppermute | solution.py:19
  85.2 0.3 convolution_bitcast_fusion.10
  86.2 2.4 %collective-permute-done.1 = f32[2,1,256]{2,0,1:T(2,128)S(1)} collective-permute-done((f32[2,1,256]{2,0,1:T(2,128)S(1)}, f32[2,1,256]{2,0,1:T(2,128)S(1)}, u32[]{:S(2)}, u32[]{:S(2)}) %collective-permute-start.1) | collective-permute-done | bytes 2080 | tf_op jit(solution)/shard_map/ppermute | solution.py:19
  88.9 0.3 convolution_bitcast_fusion.6
  89.9 2.4 %collective-permute-done.2 = f32[2,1,256]{2,0,1:T(2,128)S(1)} collective-permute-done((f32[2,1,256]{2,0,1:T(2,128)S(1)}, f32[2,1,256]{2,0,1:T(2,128)S(1)}, u32[]{:S(2)}, u32[]{:S(2)}) %collective-permute-start.2) | collective-permute-done | bytes 2080 | tf_op jit(solution)/shard_map/ppermute | solution.py:19
  92.6 0.3 convolution_bitcast_fusion.2
  92.9 0.3 fusion.20
  93.5 11.7 %all-reduce = f32[2,1,16]{2,1,0:T(1,128)S(1)} all-reduce(f32[2,1,16]{2,1,0:T(1,128)S(1)} %fusion.99), channel_id=3, replica_groups=mesh['pb'=4,'freq'=4,'ga'=2] {'pb'}, use_global_device_ids=true, to_apply=%region_3.4.clone | all-reduce | flops 32 | bytes 256
  105.3 0.6 pad_maximum_fusion.1
  (27 shorter events, 4.0 us)
Async XLA Ops:
  6.5 12.8 %copy-start = (f32[16,256]{1,0:T(8,128)S(1)}, f32[16,256]{1,0:T(8,128)}, u32[]{:S(2)}) copy-start(f32[16,256]{1,0:T(8,128)} %param.9) | copy-start | bytes 49156
  6.5 42.0 %all-gather.3.cloned.1.call-start = ((), (), s32[]{:S(2)}) async-start(), calls=%async_computation | async-start | bytes 4718592 | tf_op jit(solution)/shard_map/all_gather | solution.py:64
  81.8 3.1 %collective-permute-start = (f32[2,1,256]{2,0,1:T(2,128)S(1)}, f32[2,1,256]{2,0,1:T(2,128)S(1)}, u32[]{:S(2)}, u32[]{:S(2)}) collective-permute-start(f32[2,1,256]{2,0,1:T(2,128)S(1)} %fusion.103), channel_id=1, source_target_pairs={{6,0},{0,2},{2,4},{4,6},{7,1},{1,3},{3,5},{5,7},{14,8},{8,10},{10,... | collective-permute-start | bytes 6152 | tf_op jit(solution)/shard_map/ppermute | solution.py:19
  85.5 3.1 %collective-permute-start.1 = (f32[2,1,256]{2,0,1:T(2,128)S(1)}, f32[2,1,256]{2,0,1:T(2,128)S(1)}, u32[]{:S(2)}, u32[]{:S(2)}) collective-permute-start(f32[2,1,256]{2,0,1:T(2,128)S(1)} %collective-permute-done), channel_id=1, source_target_pairs={{6,0},{0,2},{2,4},{4,6},{7,1},{1,3},{3,5},{5,7},{14,8},{8,10},{10,... | collective-permute-start | bytes 6152 | tf_op jit(solution)/shard_map/ppermute | solution.py:19
  89.2 3.1 %collective-permute-start.2 = (f32[2,1,256]{2,0,1:T(2,128)S(1)}, f32[2,1,256]{2,0,1:T(2,128)S(1)}, u32[]{:S(2)}, u32[]{:S(2)}) collective-permute-start(f32[2,1,256]{2,0,1:T(2,128)S(1)} %collective-permute-done.1), channel_id=1, source_target_pairs={{6,0},{0,2},{2,4},{4,6},{7,1},{1,3},{3,5},{5,7},{14,8},{8,10},{10,... | collective-permute-start | bytes 6152 | tf_op jit(solution)/shard_map/ppermute | solution.py:19
Sparse Core Ops, SparseCore 0:
  9.2 39.2 all-gather.2
where the time goes:
time: 113 us
  waiting for transfers between devices  36.8 us (33%)
  matrix products  27.7 us (25%)
  between operations  18.7 us (17%)
  blocking collectives  16.6 us (15%)
  local copies, waits for them, and re-layouts  6.86 us (6%)
  other arithmetic  5.96 us (5%)
    all_gather x1, waiting for transfers between devices, body(): whole = lax.all_gather(local_block, ('freq', 'ga'), axis=1, tiled=True)  28.6 us
    dot_general x1, matrix products, panel_product(): lax.dot_general(density_all.reshape(2 * pair_rows, -1), screen.reshape(2...  22.8 us
    unnamed x1, blocking collectives  11.7 us
    ppermute x3, waiting for transfers between devices, from_behind(): return lax.ppermute(block, axis, route)  7.46 us
    psum x1, blocking collectives, body(): pair_total = lax.psum(jnp.stack([real_sum, imag_sum]), 'ga')  4.93 us
  transfers between devices with their start and end apart: 4, of which 4 were waited for; matrix products, arithmetic and copies ran while one was open for 8% of the time, Pallas kernels for 0%

commit v1 on v0

--- a/solution.py
+++ b/solution.py
@@ -1,9 +1,17 @@
+import functools
 import math
 
 import jax
 import jax.numpy as jnp
 from jax import lax
+from jax.experimental import pallas as pl
+from jax.experimental.pallas import tpu as pltpu
 from jax.sharding import PartitionSpec as P
+
+MESH = pl.DeviceIdType.MESH
+CHUNKS = 8
+TILE = 512
+AHEAD = 3
 
 NB = 256
 NS = 1
@@ -52,7 +60,7 @@
     return (product[0, :, 0] - product[1, :, 1], product[0, :, 1] + product[1, :, 0])
 
 
-def body(densities, screened, energies, occupied, kmq, offsets, weights):
+def plain_body(densities, screened, energies, occupied, kmq, offsets, weights):
     qpoint = lax.axis_index("pb")
     my_freq = lax.axis_index("freq")
     my_panel = lax.axis_index("ga")
@@ -90,6 +98,283 @@
     return jnp.stack([-prefactor * local_part[1], prefactor * local_part[0]])
 
 
+def fused_kernel(
+    shape,
+    dens_ref,
+    screen_ref,
+    energy_ref,
+    filled_ref,
+    kmq_ref,
+    offset_ref,
+    weight_ref,
+    out_ref,
+    blocks,
+    panel,
+    acc,
+    green,
+    plane_parts,
+    pb_parts,
+    own_sem,
+    panel_sem,
+    send_sem,
+    recv_sem,
+    plane_send,
+    plane_recv,
+    pb_send,
+    pb_recv,
+):
+    count_pb, count_freq, count_ga, chunks, width, tile = shape
+    group = count_freq * count_ga
+    pair_rows = blocks.shape[3]
+    pairs = group * pair_rows
+    panel_rows = panel.shape[2]
+    total_out = green.shape[2]
+    qpoint = lax.axis_index("pb")
+    freq = lax.axis_index("freq")
+    x = lax.axis_index("ga")
+    y, core = freq // 2, freq % 2
+    ny, nx, nc = 1 - y, 1 - x, 1 - core
+
+    def place(yy, cc, xx):
+        return (yy * 2 + cc) * count_ga + xx
+
+    me = place(y, core, x)
+    at_x = {"freq": freq, "ga": nx}
+    at_y = {"freq": ny * 2 + core, "ga": x}
+    at_core = {"freq": y * 2 + nc, "ga": x}
+    onward = {"freq": (y + core * (1 - 2 * y)) * 2 + core, "ga": x + (1 - core) * (1 - 2 * x)}
+    passed = place(y + (1 - core) * (1 - 2 * y), core, x + core * (1 - 2 * x))
+    from_x = place(y, core, nx)
+    from_y = place(ny, core, x)
+    across = place(ny, core, nx)
+    mine = (me, from_x, from_y, across)
+    theirs = (place(y, nc, x), place(y, nc, nx), place(ny, nc, x), place(ny, nc, nx))
+
+    def own_copy(k):
+        return pltpu.make_async_copy(
+            dens_ref.at[0, :, :, pl.ds(k * width, width)], blocks.at[k, me], own_sem.at[k]
+        )
+
+    def panel_copy(k):
+        return pltpu.make_async_copy(
+            screen_ref.at[0, 0, :, :, pl.ds(k * width, width)], panel.at[k], panel_sem.at[k]
+        )
+
+    def remote(k, lane, block, target):
+        return pltpu.make_async_remote_copy(
+            src_ref=blocks.at[k, block],
+            dst_ref=blocks.at[k, block],
+            send_sem=send_sem.at[lane, k],
+            recv_sem=recv_sem.at[lane, k],
+            device_id=target,
+            device_id_type=MESH,
+        )
+
+    for k in range(chunks):
+        own_copy(k).start()
+    for k in range(chunks):
+        panel_copy(k).start()
+
+    barrier = pltpu.get_barrier_semaphore()
+    peers = []
+    for step in range(1, group):
+        spot = (me + step) % group
+        peers.append({"freq": spot // count_ga, "ga": spot % count_ga})
+    layers = []
+    for step in range(1, count_pb):
+        layers.append({"pb": (qpoint + step) % count_pb})
+    for target in peers + layers:
+        pl.semaphore_signal(barrier, inc=1, device_id=target, device_id_type=MESH)
+    pl.semaphore_wait(barrier, len(peers) + len(layers))
+
+    def send_own(k):
+        own_copy(k).wait()
+        remote(k, 0, me, at_x).start()
+        remote(k, 1, me, at_y).start()
+        remote(k, 3, me, at_core).start()
+
+    def pass_on(k):
+        remote(k, 0, from_x, at_x).wait_recv()
+        remote(k, 1, from_y, at_y).wait_recv()
+        remote(k, 2, passed, onward).start()
+        remote(k, 4, from_x, at_core).start()
+        remote(k, 5, from_y, at_core).start()
+
+    def share_across(k):
+        remote(k, 2, across, onward).wait_recv()
+        remote(k, 6, across, at_core).start()
+
+    def arrive(k):
+        for which in range(4):
+            remote(k, 3 + which, theirs[which], at_core).wait_recv()
+        panel_copy(k).wait()
+
+    for k in range(AHEAD):
+        send_own(k)
+
+    kpoint = kmq_ref[qpoint]
+    level_row = energy_ref[pl.ds(kpoint, 1), :]
+    levels = jnp.broadcast_to(level_row, (8, level_row.shape[1])).T[:, :1]
+    bands = lax.broadcasted_iota(jnp.int32, (level_row.shape[1], total_out), 0)
+    grid = lax.broadcasted_iota(jnp.int32, (level_row.shape[1], total_out), 1)
+    omegas = -2.0 + 4.0 * grid.astype(jnp.float32) / total_out
+    freq_shift = 4.0 * offset_ref[freq].astype(jnp.float32) / total_out
+    real_part = omegas - freq_shift - levels
+    imag_part = jnp.where(bands < filled_ref[kpoint], -broadening, broadening)
+    scale = weight_ref[freq] / (2.0 * math.pi * count_pb)
+    inverse = scale / (real_part * real_part + imag_part * imag_part)
+    green[0] = real_part * inverse
+    green[1] = -imag_part * inverse
+
+    tiles = panel_rows // tile
+    pass_on(0)
+    for k in range(chunks):
+        if k + AHEAD < chunks:
+            send_own(k + AHEAD)
+        if k + 1 < chunks:
+            pass_on(k + 1)
+        share_across(k)
+        arrive(k)
+        for plane in range(2):
+
+            @pl.loop(0, tiles)
+            def _(t):
+                rows = pl.ds(pl.multiple_of(t * tile, tile), tile)
+                left = blocks[k].reshape(2 * pairs, width)
+                value = lax.dot_general(
+                    left,
+                    panel[k, plane, rows, :],
+                    (((1,), (1,)), ((), ())),
+                    preferred_element_type=jnp.float32,
+                )
+                if k == 0:
+                    acc[plane, :, rows] = value
+                else:
+                    acc[plane, :, rows] += value
+
+    chunks_here = panel_rows // width
+    spread = 128
+    sums = []
+    for b in range(group):
+        def add_chunk(t, totals):
+            real_total, imag_total = totals
+            for part in range(width // spread):
+                dense = blocks[x * chunks_here + t, b, :, :, part * spread : (part + 1) * spread]
+                dense = dense.astype(jnp.float32)
+                cols = pl.ds(pl.multiple_of(t * width, width) + part * spread, spread)
+                low = pl.ds(2 * b * pair_rows, pair_rows)
+                high = pl.ds((2 * b + 1) * pair_rows, pair_rows)
+                real_x = acc[0, low, cols] - acc[1, high, cols]
+                imag_x = acc[1, low, cols] + acc[0, high, cols]
+                real_total = real_total + dense[0] * real_x + dense[1] * imag_x
+                imag_total = imag_total + dense[0] * imag_x - dense[1] * real_x
+            return real_total, imag_total
+
+        zero = jnp.zeros((pair_rows, spread), jnp.float32)
+        sums.append(lax.fori_loop(0, chunks_here, add_chunk, (zero, zero)))
+    pair_real = jnp.sum(jnp.concatenate([s[0] for s in sums]), axis=1, keepdims=True)
+    pair_imag = jnp.sum(jnp.concatenate([s[1] for s in sums]), axis=1, keepdims=True)
+    real_out = jnp.sum(pair_real * green[0] - pair_imag * green[1], axis=0, keepdims=True)
+    imag_out = jnp.sum(pair_real * green[1] + pair_imag * green[0], axis=0, keepdims=True)
+
+    plane_parts[0, 0:1] = -imag_out
+    plane_parts[0, 1:2] = real_out
+    copies = []
+    for step in range(1, group):
+        copy = pltpu.make_async_remote_copy(
+            src_ref=plane_parts.at[0],
+            dst_ref=plane_parts.at[step],
+            send_sem=plane_send.at[step],
+            recv_sem=plane_recv.at[step],
+            device_id=peers[step - 1],
+            device_id_type=MESH,
+        )
+        copy.start()
+        copies.append(copy)
+    for copy in copies:
+        copy.wait_recv()
+    pb_parts[0] = jnp.sum(plane_parts[...], axis=0)
+    for step in range(1, count_pb):
+        copy = pltpu.make_async_remote_copy(
+            src_ref=pb_parts.at[0],
+            dst_ref=pb_parts.at[step],
+            send_sem=pb_send.at[step],
+            recv_sem=pb_recv.at[step],
+            device_id=layers[step - 1],
+            device_id_type=MESH,
+        )
+        copy.start()
+        copies.append(copy)
+    for copy in copies[group - 1 :]:
+        copy.wait_recv()
+    total = jnp.sum(pb_parts[...], axis=0)
+    first = (qpoint * count_freq + freq) * OUT_DEV
+    lanes = lax.broadcasted_iota(jnp.int32, total.shape, 1)
+    spots = lax.broadcasted_iota(jnp.int32, (2, OUT_DEV), 1)
+    result = jnp.zeros((2, OUT_DEV), jnp.float32)
+    for j in range(OUT_DEV):
+        picked = jnp.sum(jnp.where(lanes == first + j, total, 0.0), axis=1, keepdims=True)
+        result = jnp.where(spots == j, picked, result)
+    out_ref[...] = result.reshape(out_ref.shape)
+
+    for copy in copies:
+        copy.wait_send()
+    for k in range(chunks):
+        remote(k, 0, me, at_x).wait_send()
+        remote(k, 1, me, at_y).wait_send()
+        remote(k, 2, passed, onward).wait_send()
+        for which in range(4):
+            remote(k, 3 + which, mine[which], at_core).wait_send()
+
+
+def fused_body(densities, screened, energies, occupied, kmq, offsets, weights):
+    count_pb = lax.axis_size("pb")
+    count_freq = lax.axis_size("freq")
+    count_ga = lax.axis_size("ga")
+    pair_rows, basis = densities.shape[2:]
+    panel_rows = screened.shape[3]
+    group = count_freq * count_ga
+    pairs = group * pair_rows
+    width = basis // CHUNKS
+    total_out = OUT_DEV * count_pb * count_freq
+    shape = (count_pb, count_freq, count_ga, CHUNKS, width, min(TILE, panel_rows))
+    anywhere = pl.BlockSpec(memory_space=pl.ANY)
+    scalar = pl.BlockSpec(memory_space=pltpu.SMEM)
+    vector = pl.BlockSpec(memory_space=pltpu.VMEM)
+    return pl.pallas_call(
+        functools.partial(fused_kernel, shape),
+        out_shape=jax.ShapeDtypeStruct((2, NS, OUT_DEV), jnp.float32),
+        in_specs=[anywhere, anywhere, vector, scalar, scalar, scalar, scalar],
+        out_specs=vector,
+        scratch_shapes=[
+            pltpu.VMEM((CHUNKS, group, 2, pair_rows, width), jnp.bfloat16),
+            pltpu.VMEM((CHUNKS, 2, panel_rows, width), jnp.bfloat16),
+            pltpu.VMEM((2, 2 * pairs, panel_rows), jnp.float32),
+            pltpu.VMEM((2, NB, total_out), jnp.float32),
+            pltpu.VMEM((group, 2, total_out), jnp.float32),
+            pltpu.VMEM((count_pb, 2, total_out), jnp.float32),
+            pltpu.SemaphoreType.DMA((CHUNKS,)),
+            pltpu.SemaphoreType.DMA((CHUNKS,)),
+            pltpu.SemaphoreType.DMA((7, CHUNKS)),
+            pltpu.SemaphoreType.DMA((7, CHUNKS)),
+            pltpu.SemaphoreType.DMA((group,)),
+            pltpu.SemaphoreType.DMA((group,)),
+            pltpu.SemaphoreType.DMA((count_pb,)),
+            pltpu.SemaphoreType.DMA((count_pb,)),
+        ],
+        compiler_params=pltpu.CompilerParams(
+            collective_id=0, has_side_effects=True, vmem_limit_bytes=58 * 2**20
+        ),
+    )(densities, screened, energies, occupied, kmq, offsets, weights)
+
+
+def body(densities, screened, *rest):
+    chips = lax.axis_size("freq") == 4 and lax.axis_size("ga") == 2
+    if chips and densities.shape[2] % 16 == 0 and densities.shape[3] % (CHUNKS * 128) == 0:
+        return fused_body(densities, screened, *rest)
+    return plain_body(densities, screened, *rest)
+
+
 def solution(mesh):
     placed = (
         P("pb", None, ("freq", "ga"), None),

time: 113 us -> 65.1 us (0.58)
  Pallas kernels: 0 us -> 63.7 us
  waiting for transfers between devices: 36.8 us -> 0 us
  matrix products: 27.7 us -> 0 us
  between operations: 18.7 us -> 0.01 us
  blocking collectives: 16.6 us -> 0 us
  other arithmetic: 5.96 us -> 0 us
  local copies, waits for them, and re-layouts: 6.86 us -> 1.24 us
    pallas_call x0 -> x1, Pallas kernels: none -> 63.7 us  [fused_body(): pl.pallas_call(functools.partial(fused_kernel, shape), out_shape=jax.Shap...]
    all_gather x1 -> x0, waiting for transfers between devices: 28.6 us -> none  [body(): whole = lax.all_gather(local_block, ('freq', 'ga'), axis=1, tiled=True)]
    dot_general x17 -> x0, matrix products: 27.7 us -> none  [the longest x1 22.8 us: panel_product(): lax.dot_general(density_all.reshape(2 * pair_rows, -1), screen.reshape(2...]
    unnamed x1 -> x0, blocking collectives: 11.7 us -> none
    ppermute x3 -> x0, waiting for transfers between devices: 7.46 us -> none  [from_behind(): return lax.ppermute(block, axis, route)]
    dynamic_slice x5 -> x0, local copies, waits for them, and re-layouts: 5.25 us -> none  [the longest x1 1.48 us: body(): freq_shift = 4.0 * offsets[anchor].astype(jnp.float32) / total_out]
    psum x1 -> x0, blocking collectives: 4.93 us -> none  [body(): pair_total = lax.psum(jnp.stack([real_sum, imag_sum]), 'ga')]
    convert_element_type x1 -> x0, other arithmetic: 2.1 us -> none  [body(): dense = own_rows.astype(jnp.float32)]
  transfers between devices with their start and end apart: 4 -> 0, of which waited for: 4 -> 0; matrix products, arithmetic and copies ran while one was open for 8% -> 0% of each run, Pallas kernels for 0% -> 0%
where the time goes in v1:
time: 65.1 us; the launch traced here: 65 us
  Pallas kernels  63.7 us (98%)
  local copies, waits for them, and re-layouts  1.24 us (2%)
    pallas_call x1, Pallas kernels, fused_body(): pl.pallas_call(functools.partial(fused_kernel, shape), out_shape=jax.Shap...  63.7 us

profile of v1, /device:TPU:0, one launch (start us, length us, event | category | flops | bytes accessed | tf_op | source)
XLA Modules:
  0.0 65.0 jit_solution(5268297387412742045)
XLA Ops:
  0.0 63.7 %shard_map.73 = f32[2,1,4]{2,1,0:T(1,128)} custom-call(bf16[1,2,32,4096]{3,2,1,0:T(8,128)(2,1)} %dens_ref.1, bf16[1,1,2,2048,4096]{4,3,2,1,0:T(8,128)(2,1)} %screen_ref.1, f32[16,256]{1,0:T(8,128)} %energy_ref.1, s32[16]{0:T(128)} %filled_ref.1, s32[4]{0:T(128)} %kmq_ref.1, s32[4]{0:T(128)} %offset_ref.1, f32[4]{0:T(128)} %weight_ref.1), custom_call_target="tpu_custom_call" | custom-call | tf_op jit(solution)/shard_map/pallas_call | solution.py:344
  63.7 1.2 %copy.9 = f32[2,1,4]{2,1,0:T(1,128)} copy(f32[2,1,4]{2,1,0:T(1,128)} %shard_map.73) | data formatting | bytes 64

commit v2 on v1

--- a/solution.py
+++ b/solution.py
@@ -10,7 +10,7 @@
 
 MESH = pl.DeviceIdType.MESH
 CHUNKS = 8
-TILE = 512
+TILE = 2048
 AHEAD = 3
 
 NB = 256

time: 65.1 us -> 54.1 us (0.83)
  Pallas kernels: 63.7 us -> 52.6 us
    pallas_call x1, Pallas kernels: 63.7 us -> 52.6 us  [fused_body(): pl.pallas_call(functools.partial(fused_kernel, shape), out_shape=jax.Shap...]
where the time goes in v2:
time: 54.1 us; the launch traced here: 53.9 us
  Pallas kernels  52.6 us (97%)
  local copies, waits for them, and re-layouts  1.24 us (2%)
    pallas_call x1, Pallas kernels, fused_body(): pl.pallas_call(functools.partial(fused_kernel, shape), out_shape=jax.Shap...  52.6 us
    unnamed x1, local copies, waits for them, and re-layouts  1.24 us

profile of v2, /device:TPU:0, one launch (start us, length us, event | category | flops | bytes accessed | tf_op | source)
XLA Modules:
  0.0 53.9 jit_solution(18117760326101819524)
XLA Ops:
  0.0 52.6 %shard_map.73 = f32[2,1,4]{2,1,0:T(1,128)} custom-call(bf16[1,2,32,4096]{3,2,1,0:T(8,128)(2,1)} %dens_ref.1, bf16[1,1,2,2048,4096]{4,3,2,1,0:T(8,128)(2,1)} %screen_ref.1, f32[16,256]{1,0:T(8,128)} %energy_ref.1, s32[16]{0:T(128)} %filled_ref.1, s32[4]{0:T(128)} %kmq_ref.1, s32[4]{0:T(128)} %offset_ref.1, f32[4]{0:T(128)} %weight_ref.1), custom_call_target="tpu_custom_call" | custom-call | tf_op jit(solution)/shard_map/pallas_call | solution.py:344
  52.6 1.2 %copy.9 = f32[2,1,4]{2,1,0:T(1,128)} copy(f32[2,1,4]{2,1,0:T(1,128)} %shard_map.73) | data formatting | bytes 64

commit v3 on v2

--- a/solution.py
+++ b/solution.py
@@ -112,16 +112,13 @@
     panel,
     acc,
     green,
-    plane_parts,
-    pb_parts,
+    parts,
     own_sem,
     panel_sem,
     send_sem,
     recv_sem,
-    plane_send,
-    plane_recv,
-    pb_send,
-    pb_recv,
+    part_send,
+    part_recv,
 ):
     count_pb, count_freq, count_ga, chunks, width, tile = shape
     group = count_freq * count_ga
@@ -177,15 +174,13 @@
 
     barrier = pltpu.get_barrier_semaphore()
     peers = []
-    for step in range(1, group):
+    for step in range(1, count_pb * group):
+        layer = (qpoint + step // group) % count_pb
         spot = (me + step) % group
-        peers.append({"freq": spot // count_ga, "ga": spot % count_ga})
-    layers = []
-    for step in range(1, count_pb):
-        layers.append({"pb": (qpoint + step) % count_pb})
-    for target in peers + layers:
+        peers.append({"pb": layer, "freq": spot // count_ga, "ga": spot % count_ga})
+    for target in peers:
         pl.semaphore_signal(barrier, inc=1, device_id=target, device_id_type=MESH)
-    pl.semaphore_wait(barrier, len(peers) + len(layers))
+    pl.semaphore_wait(barrier, len(peers))
 
     def send_own(k):
         own_copy(k).wait()
@@ -228,14 +223,18 @@
 
     tiles = panel_rows // tile
     pass_on(0)
+    pass_on(1)
+    share_across(0)
     for k in range(chunks):
         if k + AHEAD < chunks:
             send_own(k + AHEAD)
-        if k + 1 < chunks:
-            pass_on(k + 1)
-        share_across(k)
         arrive(k)
         for plane in range(2):
+            if plane == 1:
+                if k + 2 < chunks:
+                    pass_on(k + 2)
+                if k + 1 < chunks:
+                    share_across(k + 1)
 
             @pl.loop(0, tiles)
             def _(t):
@@ -277,37 +276,23 @@
     real_out = jnp.sum(pair_real * green[0] - pair_imag * green[1], axis=0, keepdims=True)
     imag_out = jnp.sum(pair_real * green[1] + pair_imag * green[0], axis=0, keepdims=True)
 
-    plane_parts[0, 0:1] = -imag_out
-    plane_parts[0, 1:2] = real_out
+    parts[0, 0:1] = -imag_out
+    parts[0, 1:2] = real_out
     copies = []
-    for step in range(1, group):
+    for step, target in enumerate(peers, 1):
         copy = pltpu.make_async_remote_copy(
-            src_ref=plane_parts.at[0],
-            dst_ref=plane_parts.at[step],
-            send_sem=plane_send.at[step],
-            recv_sem=plane_recv.at[step],
-            device_id=peers[step - 1],
+            src_ref=parts.at[0],
+            dst_ref=parts.at[step],
+            send_sem=part_send.at[step],
+            recv_sem=part_recv.at[step],
+            device_id=target,
             device_id_type=MESH,
         )
         copy.start()
         copies.append(copy)
     for copy in copies:
         copy.wait_recv()
-    pb_parts[0] = jnp.sum(plane_parts[...], axis=0)
-    for step in range(1, count_pb):
-        copy = pltpu.make_async_remote_copy(
-            src_ref=pb_parts.at[0],
-            dst_ref=pb_parts.at[step],
-            send_sem=pb_send.at[step],
-            recv_sem=pb_recv.at[step],
-            device_id=layers[step - 1],
-            device_id_type=MESH,
-        )
-        copy.start()
-        copies.append(copy)
-    for copy in copies[group - 1 :]:
-        copy.wait_recv()
-    total = jnp.sum(pb_parts[...], axis=0)
+    total = jnp.sum(parts[...], axis=0)
     first = (qpoint * count_freq + freq) * OUT_DEV
     lanes = lax.broadcasted_iota(jnp.int32, total.shape, 1)
     spots = lax.broadcasted_iota(jnp.int32, (2, OUT_DEV), 1)
@@ -351,16 +336,13 @@
             pltpu.VMEM((CHUNKS, 2, panel_rows, width), jnp.bfloat16),
             pltpu.VMEM((2, 2 * pairs, panel_rows), jnp.float32),
             pltpu.VMEM((2, NB, total_out), jnp.float32),
-            pltpu.VMEM((group, 2, total_out), jnp.float32),
-            pltpu.VMEM((count_pb, 2, total_out), jnp.float32),
+            pltpu.VMEM((count_pb * group, 2, total_out), jnp.float32),
             pltpu.SemaphoreType.DMA((CHUNKS,)),
             pltpu.SemaphoreType.DMA((CHUNKS,)),
             pltpu.SemaphoreType.DMA((7, CHUNKS)),
             pltpu.SemaphoreType.DMA((7, CHUNKS)),
-            pltpu.SemaphoreType.DMA((group,)),
-            pltpu.SemaphoreType.DMA((group,)),
-            pltpu.SemaphoreType.DMA((count_pb,)),
-            pltpu.SemaphoreType.DMA((count_pb,)),
+            pltpu.SemaphoreType.DMA((count_pb * group,)),
+            pltpu.SemaphoreType.DMA((count_pb * group,)),
         ],
         compiler_params=pltpu.CompilerParams(
             collective_id=0, has_side_effects=True, vmem_limit_bytes=58 * 2**20

time: 54.1 us -> 47.4 us (0.88)
  Pallas kernels: 52.6 us -> 46 us
    pallas_call x1, Pallas kernels: 52.6 us -> 46 us  [fused_body(): pl.pallas_call(functools.partial(fused_kernel, shape), out_shape=jax.Shap...]
where the time goes in v3:
time: 47.4 us; the launch traced here: 47.2 us
  Pallas kernels  46 us (97%)
  local copies, waits for them, and re-layouts  1.24 us (3%)
    pallas_call x1, Pallas kernels, fused_body(): pl.pallas_call(functools.partial(fused_kernel, shape), out_shape=jax.Shap...  46 us
    unnamed x1, local copies, waits for them, and re-layouts  1.24 us

profile of v3, /device:TPU:0, one launch (start us, length us, event | category | flops | bytes accessed | tf_op | source)
XLA Modules:
  0.0 47.2 jit_solution(2541496558291097743)
XLA Ops:
  0.0 46.0 %shard_map.73 = f32[2,1,4]{2,1,0:T(1,128)} custom-call(bf16[1,2,32,4096]{3,2,1,0:T(8,128)(2,1)} %dens_ref.1, bf16[1,1,2,2048,4096]{4,3,2,1,0:T(8,128)(2,1)} %screen_ref.1, f32[16,256]{1,0:T(8,128)} %energy_ref.1, s32[16]{0:T(128)} %filled_ref.1, s32[4]{0:T(128)} %kmq_ref.1, s32[4]{0:T(128)} %offset_ref.1, f32[4]{0:T(128)} %weight_ref.1), custom_call_target="tpu_custom_call" | custom-call | tf_op jit(solution)/shard_map/pallas_call | solution.py:329
  46.0 1.2 %copy.9 = f32[2,1,4]{2,1,0:T(1,128)} copy(f32[2,1,4]{2,1,0:T(1,128)} %shard_map.73) | data formatting | bytes 64

commit v4 on v3

--- a/solution.py
+++ b/solution.py
@@ -11,7 +11,7 @@
 MESH = pl.DeviceIdType.MESH
 CHUNKS = 8
 TILE = 2048
-AHEAD = 3
+AHEAD = 4
 
 NB = 256
 NS = 1
@@ -119,6 +119,7 @@
     recv_sem,
     part_send,
     part_recv,
+    ready,
 ):
     count_pb, count_freq, count_ga, chunks, width, tile = shape
     group = count_freq * count_ga
@@ -178,9 +179,11 @@
         layer = (qpoint + step // group) % count_pb
         spot = (me + step) % group
         peers.append({"pb": layer, "freq": spot // count_ga, "ga": spot % count_ga})
-    for target in peers:
+    layers = [{"pb": (qpoint + step) % count_pb} for step in range(1, count_pb)]
+    near = [at_x, at_y, at_core] + layers
+    for target in near:
         pl.semaphore_signal(barrier, inc=1, device_id=target, device_id_type=MESH)
-    pl.semaphore_wait(barrier, len(peers))
+    pl.semaphore_wait(barrier, len(near))
 
     def send_own(k):
         own_copy(k).wait()
@@ -228,11 +231,14 @@
     for k in range(chunks):
         if k + AHEAD < chunks:
             send_own(k + AHEAD)
+        if k + 2 < chunks:
+            pass_on(k + 2)
         arrive(k)
+        if k == chunks - 2:
+            for target in layers:
+                pl.semaphore_signal(ready, inc=1, device_id=target, device_id_type=MESH)
         for plane in range(2):
             if plane == 1:
-                if k + 2 < chunks:
-                    pass_on(k + 2)
                 if k + 1 < chunks:
                     share_across(k + 1)
 
@@ -278,6 +284,7 @@
 
     parts[0, 0:1] = -imag_out
     parts[0, 1:2] = real_out
+    pl.semaphore_wait(ready, len(layers))
     copies = []
     for step, target in enumerate(peers, 1):
         copy = pltpu.make_async_remote_copy(
@@ -343,6 +350,7 @@
             pltpu.SemaphoreType.DMA((7, CHUNKS)),
             pltpu.SemaphoreType.DMA((count_pb * group,)),
             pltpu.SemaphoreType.DMA((count_pb * group,)),
+            pltpu.SemaphoreType.REGULAR,
         ],
         compiler_params=pltpu.CompilerParams(
             collective_id=0, has_side_effects=True, vmem_limit_bytes=58 * 2**20

time: 47.4 us -> 46.2 us (0.975)
  Pallas kernels: 46 us -> 44.8 us
    pallas_call x1, Pallas kernels: 46 us -> 44.8 us  [fused_body(): pl.pallas_call(functools.partial(fused_kernel, shape), out_shape=jax.Shap...]
where the time goes in v4:
time: 46.2 us; the launch traced here: 46 us
  Pallas kernels  44.8 us (97%)
  local copies, waits for them, and re-layouts  1.24 us (3%)
    pallas_call x1, Pallas kernels, fused_body(): pl.pallas_call(functools.partial(fused_kernel, shape), out_shape=jax.Shap...  44.8 us
    unnamed x1, local copies, waits for them, and re-layouts  1.24 us

profile of v4, /device:TPU:0, one launch (start us, length us, event | category | flops | bytes accessed | tf_op | source)
XLA Modules:
  0.0 46.0 jit_solution(13572493375992274805)
XLA Ops:
  0.0 44.8 %shard_map.73 = f32[2,1,4]{2,1,0:T(1,128)} custom-call(bf16[1,2,32,4096]{3,2,1,0:T(8,128)(2,1)} %dens_ref.1, bf16[1,1,2,2048,4096]{4,3,2,1,0:T(8,128)(2,1)} %screen_ref.1, f32[16,256]{1,0:T(8,128)} %energy_ref.1, s32[16]{0:T(128)} %filled_ref.1, s32[4]{0:T(128)} %kmq_ref.1, s32[4]{0:T(128)} %offset_ref.1, f32[4]{0:T(128)} %weight_ref.1), custom_call_target="tpu_custom_call" | custom-call | tf_op jit(solution)/shard_map/pallas_call | solution.py:336
  44.8 1.2 %copy.9 = f32[2,1,4]{2,1,0:T(1,128)} copy(f32[2,1,4]{2,1,0:T(1,128)} %shard_map.73) | data formatting | bytes 64
